TPU v7x, 32 devices: a whole 2x2x4 slice. The times are simulated.
32 devices in a mesh: dp: 16 (over z, x, core), tensor: 2 (over y).
Axes of the slice: x: 2, y: 2, z: 4, core: 2. Of those that a mesh axis runs over, the one named last changes fastest.
Arguments:
- grad_hidden: bfloat16 [2048, 14336], P('dp', 'tensor'), may hold values from -18 to 18
- gate: bfloat16 [2048, 14336], P('dp', 'tensor'), may hold values from -6 to 6
Outputs:
- factor: float32 [14336, 14336], P('tensor', 'dp')
All inputs are finite; a program needn't handle non-finite values.
Results may differ from a plain program's by a relative error of at most 0.0065.
Values may be sent and summed in bfloat16 or wider, within the bound.
A program may use at most 128 MiB of HBM per device.

v0:
```python
import functools

import jax
import jax.numpy as jnp
from jax import lax
from jax.experimental import pallas as pl
from jax.experimental.pallas import tpu as pltpu
from jax.sharding import PartitionSpec as P

MESH = pl.DeviceIdType.MESH
LANES = 128


def activations(grad_hidden, gate):
    return (grad_hidden.astype(jnp.float32) * jax.nn.silu(gate.astype(jnp.float32))).astype(
        jnp.bfloat16
    )


def plain(grad_hidden, gate):
    up_grad = activations(grad_hidden, gate)
    tensor_count = lax.axis_size("tensor")
    data_count = lax.axis_size("dp")
    col_width = up_grad.shape[1] * tensor_count // data_count
    ratio = data_count // tensor_count
    data_index = lax.axis_index("dp")
    owner = data_index // ratio
    offset = data_index % ratio * col_width
    contract = (((0,), (0,)), ((), ()))
    total_tokens = up_grad.shape[0] * data_count
    rows_all = lax.all_gather(up_grad, "dp", axis=0, tiled=True)
    panel = lax.dynamic_slice_in_dim(rows_all, offset, col_width, 1)
    slices = lax.all_gather(panel, "tensor", axis=1, tiled=True)
    cols_all = lax.dynamic_slice_in_dim(slices, owner * col_width, col_width, 1)
    summed = lax.dot_general(rows_all, cols_all, contract, preferred_element_type=jnp.float32)
    return summed / total_tokens


def flip_kernel(g_ref, v_ref, o_ref):
    v = v_ref[...].astype(jnp.float32)
    u = g_ref[...].astype(jnp.float32) * (v / (1.0 + jnp.exp(-v)))
    o_ref[...] = u.astype(jnp.bfloat16).T


def flip(grad_hidden, gate, width):
    tokens, hidden = grad_hidden.shape
    return pl.pallas_call(
        flip_kernel,
        grid=(hidden // width,),
        in_specs=[pl.BlockSpec((tokens, width), lambda i: (0, i))] * 2,
        out_specs=pl.BlockSpec((width, tokens), lambda i: (i, 0)),
        out_shape=jax.ShapeDtypeStruct((hidden, tokens), jnp.bfloat16),
    )(grad_hidden, gate)


def early(line, z, x):
    end, low, high = (z == 0) | (z == line - 1), z == 0, z == line - 1
    near = jnp.where(low, 1, z - 1)
    after = jnp.where(low, 2, jnp.where(high, line - 3, z + 1))
    inner = jnp.where(z < line - 2, z + 2, z - 2) * 2 + x
    far = jnp.where(low, 3, line - 4) * 2 + x
    other = near * 2 + 1 - x
    five = [z * 2 + x, z * 2 + 1 - x, near * 2 + x, after * 2 + x, jnp.where(end, other, inner)]
    return five + [jnp.where(end, far, other)]


def member(q, chosen):
    return functools.reduce(jnp.logical_or, [q == c for c in chosen])


def late(line, z, x):
    chosen = early(line, z, x)
    left = 2 * line - len(chosen)
    picked, rank = [jnp.int32(0)] * left, jnp.int32(0)
    for q in range(2 * line):
        free = jnp.logical_not(member(q, chosen))
        picked = [jnp.where(free & (rank == j), q, p) for j, p in enumerate(picked)]
        rank = rank + free.astype(jnp.int32)
    return picked


def nt_dot(a, b):
    return lax.dot_general(a, b, (((1,), (1,)), ((), ())), preferred_element_type=jnp.float32)


def gather_kernel(
    dims, own_ref, all_ref, panel_ref, part_ref, own_sem, z_send, x_send, c_send, y_send,
    recv, c_recv, y_recv, a_ref, b_ref, a_sem, b_sem,
):
    line, count, cross, rows = dims
    first = count - cross
    me, t = lax.axis_index("dp"), lax.axis_index("tensor")
    z, x, core = me // 4, me // 2 % 2, me % 2
    chips = 2 * line
    at = lambda zz, xx: zz * 2 + xx
    here = at(z, x)
    owns = (here // (chips // 2)) == t
    part = here % (chips // 2)
    per = count // (chips // 2)

    up = (jnp.minimum(z + 1, line - 1) * 4 + x * 2 + core, t)
    down = (jnp.maximum(z - 1, 0) * 4 + x * 2 + core, t)
    over = (z * 4 + (1 - x) * 2 + core, t)
    twin = (z * 4 + x * 2 + 1 - core, t)
    has_up, has_down = z < line - 1, z > 0

    barrier = pltpu.get_barrier_semaphore()
    greet = lambda dev: pl.semaphore_signal(barrier, inc=1, device_id=dev, device_id_type=MESH)
    greet(over)
    greet(twin)
    greet((me, 1 - t))
    greet(twin[:1] + (1 - t,))
    pl.when(has_up)(lambda: greet(up))
    pl.when(has_down)(lambda: greet(down))
    end = (z == 0) | (z == line - 1)
    pl.semaphore_wait(barrier, jnp.where(end, 5, 6))

    def rows_of(k):
        return pl.ds(pl.multiple_of(k * rows, rows), rows)

    def lanes_of(q):
        return pl.ds(pl.multiple_of((q * 2 + core) * LANES, LANES), LANES)

    def place(q, k):
        return all_ref.at[rows_of(k), lanes_of(q)]

    def source(q, k, own):
        return own_ref.at[rows_of(k)] if own else place(q, k)

    def along(q, k, way, own=False):
        return pltpu.make_async_remote_copy(
            src_ref=source(q, k, own), dst_ref=place(q, k), send_sem=z_send.at[way, q, k],
            recv_sem=recv.at[q, k], device_id=(down, up)[way], device_id_type=MESH)

    def across(q, k, own=False):
        return pltpu.make_async_remote_copy(
            src_ref=source(q, k, own), dst_ref=place(q, k), send_sem=x_send.at[q, k],
            recv_sem=recv.at[q, k], device_id=over, device_id_type=MESH)

    def to_twin(q, k, own=False):
        return pltpu.make_async_remote_copy(
            src_ref=source(q, k, own), dst_ref=place(q, k), send_sem=c_send.at[q, k],
            recv_sem=c_recv.at[q, k], device_id=twin, device_id_type=MESH)

    def to_panel(q, k, own=False):
        j = k % per
        half = per // 2
        return pltpu.make_async_remote_copy(
            src_ref=source(q, k, own),
            dst_ref=panel_ref.at[rows_of(j % half), lanes_of(q)],
            send_sem=y_send.at[q, j], recv_sem=y_recv.at[q * 2 + core, j % half],
            device_id=(here * 2 + j // half, 1 - t), device_id_type=MESH)

    def spread(q, k, own=False):
        to_twin(q, k, own).start()
        pl.when(owns & (k // per == part))(lambda: to_panel(q, k, own).start())

    def arrive(q, k):
        across(q, k).wait_recv()

    keep = pltpu.make_async_copy(own_ref, all_ref.at[:, lanes_of(here)], own_sem)

    @pl.loop(0, count)
    def _(k):
        pl.when(has_up)(lambda: along(here, k, 1, True).start())
        pl.when(has_down)(lambda: along(here, k, 0, True).start())
        across(here, k, True).start()
        spread(here, k, True)

    keep.start()

    def from_line(s, k, way):
        zz = z - s if way else z + s
        valid = (zz >= 0) & (zz < line)

        @pl.when(valid)
        def _():
            q = at(zz, x)
            arrive(q, k)
            pl.when(has_up if way else has_down)(lambda: along(q, k, way).start())
            pl.when(k < first)(lambda: across(q, k).start())
            spread(q, k)

    def from_cross(s, k, way):
        zz = z - s if way else z + s
        valid = (zz >= 0) & (zz < line)

        @pl.when(valid)
        def _():
            q = at(zz, 1 - x)
            arrive(q, k)
            pl.when(has_up if way else has_down)(lambda: along(q, k, way).start())
            spread(q, k)

    def relayed(s, k):
        for zz in (z - s, z + s):
            @pl.when((zz >= 0) & (zz < line))
            def _():
                q = at(zz, 1 - x)
                arrive(q, k)
                spread(q, k)

    def pair_of(q):
        return pl.ds(pl.multiple_of(q * 2 * LANES, 2 * LANES), 2 * LANES)

    def slab(j):
        return pl.ds(j * 2 * LANES, 2 * LANES)

    chosen = early(line, z, x)
    first_group, second_group = chosen[:-1], chosen[-1:]

    def tile_copies(group, k, slot):
        return [
            pltpu.make_async_copy(
                all_ref.at[rows_of(k), pair_of(q)], a_ref.at[slot, :, slab(j)], a_sem.at[slot, j]
            )
            for j, q in enumerate(group)
        ]

    def prepare(group):
        for q in group:
            @pl.loop(0, count)
            def _(k):
                to_twin(q, k).wait_recv()
            panel_arrived(q)
        for tile in tile_copies(group, 0, 0):
            tile.start()
        for ours in (True, False):
            @pl.when(owns == ours)
            def _():
                width = rows * per // 2
                from_ref = (
                    all_ref.at[pl.ds(pl.multiple_of((part * 2 + core) * width, width), width)]
                    if ours else panel_ref
                )
                copies = [
                    pltpu.make_async_copy(from_ref.at[:, pair_of(q)], b_ref.at[:, slab(j)], b_sem.at[j])
                    for j, q in enumerate(group)
                ]
                for copy in copies:
                    copy.start()
                for copy in copies:
                    copy.wait()

    def multiply(group, k, add):
        slot = k % 2

        @pl.when(k + 1 < count)
        def _():
            for tile in tile_copies(group, k + 1, 1 - slot):
                tile.start()

        for tile in tile_copies(group, k, slot):
            tile.wait()
        span = pl.ds(0, len(group) * 2 * LANES)
        product = nt_dot(a_ref[slot, :, span], b_ref[:, span])
        if add:
            product += part_ref[rows_of(k), :]
        part_ref[rows_of(k), :] = product

    def panel_arrived(q):
        @pl.when(jnp.logical_not(owns))
        def _():
            @pl.loop(0, per // 2)
            def _(j):
                for c in range(2):
                    piece = panel_ref.at[rows_of(j), pl.ds(pl.multiple_of((q * 2 + c) * LANES, LANES), LANES)]
                    pltpu.make_async_copy(piece, piece, y_recv.at[q * 2 + c, j]).wait()

    for s in range(1, line + 2):
        if s == 3:
            keep.wait()
            prepare(first_group)
        if s == 4:
            prepare(second_group)

        @pl.loop(0, count)
        def _(k):
            if s == 3:
                multiply(first_group, k, False)
            if s == 4:
                multiply(second_group, k, True)
            if s < line:
                from_line(s, k, 1)
                from_line(s, k, 0)
            if s == 1:
                q = at(z, 1 - x)
                arrive(q, k)
                spread(q, k)
            else:
                @pl.when(k < first)
                def _():
                    if s - 1 < line:
                        pl.when(end)(lambda: relayed(s - 1, k))
                    if 1 <= s - 2 < line:
                        pl.when(jnp.logical_not(end))(lambda: relayed(s - 2, k))

        if s <= line:
            @pl.loop(first, count)
            def _(k):
                if s == 1:
                    q = at(z, 1 - x)
                    pl.when(has_up)(lambda: along(q, k, 1).start())
                    pl.when(has_down)(lambda: along(q, k, 0).start())
                else:
                    from_cross(s - 1, k, 1)
                    from_cross(s - 1, k, 0)

    @pl.loop(0, chips)
    def _(q):
        @pl.when(jnp.logical_not(member(q, chosen)))
        def _():
            @pl.loop(0, count)
            def _(k):
                to_twin(q, k).wait_recv()
            panel_arrived(q)

    @pl.loop(0, chips)
    def _(q):
        zz, mine = q // 2, q % 2 == x

        @pl.loop(0, count)
        def _(k):
            to_twin(q, k).wait_send()
            pl.when(mine & ((k < first) | (zz == z)))(lambda: across(q, k).wait_send())
            goes = mine | (k >= first)
            pl.when(goes & has_up & (zz <= z))(lambda: along(q, k, 1).wait_send())
            pl.when(goes & has_down & (zz >= z))(lambda: along(q, k, 0).wait_send())
            pl.when(owns & (k // per == part))(lambda: to_panel(q, k).wait_send())


def gather(own, dims, width, tokens):
    line, count, cross, rows = dims
    chips = 2 * line
    per = count // line
    sem = pltpu.SemaphoreType.DMA
    hidden = own.shape[0]
    return pl.pallas_call(
        functools.partial(gather_kernel, dims),
        out_shape=(
            jax.ShapeDtypeStruct((hidden, tokens), jnp.bfloat16),
            jax.ShapeDtypeStruct((width, tokens), jnp.bfloat16),
            pltpu.VMEM((hidden, width), jnp.float32),
        ),
        in_specs=[pl.BlockSpec(memory_space=pl.ANY)],
        out_specs=(
            pl.BlockSpec(memory_space=pl.ANY),
            pl.BlockSpec(memory_space=pl.ANY),
            pl.BlockSpec(memory_space=pltpu.VMEM),
        ),
        scratch_shapes=[
            sem(()),
            sem((2, chips, count)),
            sem((chips, count)),
            sem((chips, count)),
            sem((chips, per)),
            sem((chips, count)),
            sem((chips, count)),
            sem((2 * chips, per // 2)),
            pltpu.VMEM((2, rows, 10 * LANES), jnp.bfloat16),
            pltpu.VMEM((width, 10 * LANES), jnp.bfloat16),
            sem((2, 5)),
            sem((5,)),
        ],
        compiler_params=pltpu.CompilerParams(
            collective_id=0, has_side_effects=True, vmem_limit_bytes=36 * 2**20
        ),
    )(own)


def matmul_kernel(total, width, left, chips_ref, *refs):
    pieces, (all_ref, panel_ref, part_ref, o_ref, b_ref, sem) = refs[:left], refs[left:]
    me, t = lax.axis_index("dp"), lax.axis_index("tensor")
    ratio = lax.axis_size("dp") // lax.axis_size("tensor")
    step, tile = pl.program_id(0), o_ref.shape[0]

    @pl.when(step == 0)
    def _():
        for ours in (True, False):
            @pl.when((me // ratio == t) == ours)
            def _():
                rows = pl.ds(pl.multiple_of(me % ratio * width, LANES), width)
                from_ref = all_ref.at[rows] if ours else panel_ref
                copies = [
                    pltpu.make_async_copy(
                        from_ref.at[:, pl.ds(pl.multiple_of(chips_ref[j] * 2 * LANES, LANES), 2 * LANES)],
                        b_ref.at[:, pl.ds(j * 2 * LANES, 2 * LANES)],
                        sem.at[j],
                    )
                    for j in range(left)
                ]
                for copy in copies:
                    copy.start()
                for copy in copies:
                    copy.wait()

    a = jnp.concatenate([piece[...] for piece in pieces], axis=1)
    done = part_ref[pl.ds(pl.multiple_of(step * tile, tile), tile), :]
    o_ref[...] = (done + nt_dot(a, b_ref[...])) * (1.0 / total)


def matmul(everything, panel, part, chips, tile):
    hidden, tokens = everything.shape
    width = panel.shape[0]
    left = chips.shape[0]
    everything = pltpu.with_memory_space_constraint(everything, pltpu.HBM)
    panel = pltpu.with_memory_space_constraint(panel, pltpu.HBM)
    part = pltpu.with_memory_space_constraint(part, pltpu.VMEM)

    def piece(j):
        return pl.BlockSpec((tile, 2 * LANES), lambda i, chips_ref: (i, chips_ref[j]))

    return pl.pallas_call(
        functools.partial(matmul_kernel, tokens, width, left),
        grid_spec=pltpu.PrefetchScalarGridSpec(
            num_scalar_prefetch=1,
            grid=(hidden // tile,),
            in_specs=[piece(j) for j in range(left)] + [
                pl.BlockSpec(memory_space=pltpu.HBM),
                pl.BlockSpec(memory_space=pltpu.HBM),
                pl.BlockSpec(memory_space=pltpu.VMEM),
            ],
            out_specs=pl.BlockSpec((tile, width), lambda i, chips_ref: (i, 0)),
            scratch_shapes=[
                pltpu.VMEM((width, left * 2 * LANES), jnp.bfloat16),
                pltpu.SemaphoreType.DMA((left,)),
            ],
        ),
        out_shape=jax.ShapeDtypeStruct((hidden, width), jnp.float32),
        compiler_params=pltpu.CompilerParams(vmem_limit_bytes=36 * 2**20),
    )(chips, *[everything] * (left + 1), panel, part)


def shards(grad_hidden, gate):
    tensor_count, data_count = lax.axis_size("tensor"), lax.axis_size("dp")
    mine, hidden = grad_hidden.shape
    width = hidden * tensor_count // data_count
    tokens = mine * data_count
    count = data_count
    fits = (
        tensor_count == 2 and data_count % 4 == 0 and data_count >= 16 and mine == LANES and width % LANES == 0
        and hidden % (16 * count) == 0 and tokens & (tokens - 1) == 0 and hidden % 1024 == 0
    )
    if not fits:
        return plain(grad_hidden, gate)
    line = data_count // 4
    cross = round(count / (2 * (line - 1)))
    dims = (line, count, cross, hidden // count)
    own = flip(grad_hidden, gate, 1024)
    everything, panel, part = gather(own, dims, width, tokens)
    index = lax.axis_index("dp")
    chips = jnp.stack(late(line, index // 4, index // 2 % 2)).astype(jnp.int32)
    return matmul(everything, panel, part, chips, 512)


def solution(mesh):
    return jax.shard_map(
        shards,
        mesh=mesh,
        in_specs=(P("dp", "tensor"), P("dp", "tensor")),
        out_specs=P("tensor", "dp"),
        check_vma=False,
    )
```

profile of v0, /device:TPU:27, one launch (start us, length us, event | category | flops | bytes accessed | tf_op | source)
XLA Modules:
  0.0 196.2 jit_solution(15371670837711345136)
XLA Ops:
  0.0 0.6 pad_add_fusion.chips_ref
  0.6 6.1 %shard_map.28.own_ref = bf16[7168,128]{1,0:T(8,128)(2,1)} custom-call(bf16[128,7168]{1,0:T(8,128)(2,1)} %g_ref.1, bf16[128,7168]{1,0:T(8,128)(2,1)} %v_ref.1), custom_call_target="tpu_custom_call" | custom-call | tf_op jit(solution)/shard_map/pallas_call | solution.py:47
  6.7 169.8 %shard_map.29 = (bf16[7168,2048]{1,0:T(8,128)(2,1)}, bf16[896,2048]{1,0:T(8,128)(2,1)}, f32[7168,896]{1,0:T(8,128)S(1)}) custom-call(bf16[7168,128]{1,0:T(8,128)(2,1)} %shard_map.28.own_ref), custom_call_target="tpu_custom_call" | custom-call | tf_op jit(solution)/shard_map/pallas_call | solution.py:338
  176.6 19.6 %shard_map.30 = f32[7168,896]{1,0:T(8,128)} custom-call(s32[2]{0:T(128)} %pad_add_fusion.chips_ref, bf16[7168,2048]{1,0:T(8,128)(2,1)} %get-tuple-element.8.refs_0_.refs_1_.refs_2_, bf16[7168,2048]{1,0:T(8,128)(2,1)} %get-tuple-element.8.refs_0_.refs_1_.refs_2_, bf16[7168,2048]{1,0:T(8,128)(2,1)} %get-tuple-element.8.refs_0_.refs_1_.refs_2_, ...), custom_call_target="tpu_custom_call" | custom-call | tf_op jit(solution)/shard_map/pallas_call | solution.py:413
where the time goes:
time: 197 us; the launch traced here: 196 us
  Pallas kernels  196 us (99%)
    pallas_call x1, Pallas kernels, gather(): pl.pallas_call(functools.partial(gather_kernel, dims), out_shape=(jax.Sha...  170 us
    pallas_call x1, Pallas kernels, matmul(): pl.pallas_call(functools.partial(matmul_kernel, tokens, width, left), gri...  19.6 us
    pallas_call x1, Pallas kernels, flip(): pl.pallas_call(flip_kernel, grid=(hidden // width,), in_specs=[pl.BlockSp...  6.14 us

commit v1 on v0

v1 whole, which is shorter than its diff:
```python
import functools

import jax
import jax.numpy as jnp
from jax import lax
from jax.experimental import pallas as pl
from jax.experimental.pallas import tpu as pltpu
from jax.sharding import PartitionSpec as P

MESH = pl.DeviceIdType.MESH
LANES = 128
LINE = 4
CHIPS = 2 * LINE
VMEM_BYTES = 67_043_328

BOTTOM = {
    0: [(0, 0), (0, 1), (1, 0), (2, 0), (1, 1), (3, 0), (2, 1), (3, 1)],
    1: [(1, 0), (1, 1), (0, 0), (2, 0), (3, 0), (0, 1), (2, 1), (3, 1)],
}
ORDER = [BOTTOM[z] if z in BOTTOM else [(LINE - 1 - a, r) for a, r in BOTTOM[LINE - 1 - z]] for z in range(LINE)]
FIRST, SECOND = range(0, 5), range(5, 7)
LAST = CHIPS - 1


def activations(grad_hidden, gate):
    return (grad_hidden.astype(jnp.float32) * jax.nn.silu(gate.astype(jnp.float32))).astype(
        jnp.bfloat16
    )


def plain(grad_hidden, gate):
    up_grad = activations(grad_hidden, gate)
    tensor_count = lax.axis_size("tensor")
    data_count = lax.axis_size("dp")
    col_width = up_grad.shape[1] * tensor_count // data_count
    ratio = data_count // tensor_count
    data_index = lax.axis_index("dp")
    owner = data_index // ratio
    offset = data_index % ratio * col_width
    contract = (((0,), (0,)), ((), ()))
    total_tokens = up_grad.shape[0] * data_count
    rows_all = lax.all_gather(up_grad, "dp", axis=0, tiled=True)
    panel = lax.dynamic_slice_in_dim(rows_all, offset, col_width, 1)
    slices = lax.all_gather(panel, "tensor", axis=1, tiled=True)
    cols_all = lax.dynamic_slice_in_dim(slices, owner * col_width, col_width, 1)
    summed = lax.dot_general(rows_all, cols_all, contract, preferred_element_type=jnp.float32)
    return summed / total_tokens


def pick(index, values):
    known = [v for v in values if v is not None]
    if all(v == known[0] for v in known):
        return jnp.int32(known[0])
    out = jnp.int32(known[-1])
    for j, v in enumerate(values):
        if v is not None and v != known[-1]:
            out = jnp.where(index == j, v, out)
    return out


def slot_at(z, shift, d, r):
    def one(zz):
        if not (0 <= zz + d < LINE and 0 <= zz + shift < LINE):
            return None
        return ORDER[zz + shift].index((zz + d, r))
    return pick(z, [one(zz) for zz in range(LINE)])


def nt_dot(a, b):
    return lax.dot_general(a, b, (((1,), (1,)), ((), ())), preferred_element_type=jnp.float32)


def position():
    me, t = lax.axis_index("dp"), lax.axis_index("tensor")
    return me, t, me // 4, me // 2 % 2, me % 2


def gather_kernel(
    dims, g_ref, v_ref, all_ref, panel_ref, part_ref, g_buf, v_buf, g_sem, v_sem,
    z_send, x_send, c_send, y_send, recv, c_recv, y_recv,
):
    count, rows = dims
    me, t, z, x, core = position()
    here = me // 2
    half = CHIPS // 2
    owns = here // half == t
    part = here % half
    end = (z == 0) | (z == LINE - 1)
    has_up, has_down = z < LINE - 1, z > 0

    up = (jnp.minimum(z + 1, LINE - 1) * 4 + x * 2 + core, t)
    down = (jnp.maximum(z - 1, 0) * 4 + x * 2 + core, t)
    over = (z * 4 + (1 - x) * 2 + core, t)
    twin = (z * 4 + x * 2 + 1 - core, t)

    def chunk(i):
        return jnp.where(t == 0, i, count - 1 - i)

    def rows_of(k):
        return pl.ds(pl.multiple_of(k * rows, rows), rows)

    def inputs(i):
        columns = rows_of(chunk(i))
        return [
            pltpu.make_async_copy(src.at[:, columns], dst.at[:, columns], sem.at[i])
            for src, dst, sem in ((g_ref, g_buf, g_sem), (v_ref, v_buf, v_sem))
        ]

    @pl.loop(0, count)
    def _(i):
        for copy in inputs(i):
            copy.start()

    barrier = pltpu.get_barrier_semaphore()
    greet = lambda dev: pl.semaphore_signal(barrier, inc=1, device_id=dev, device_id_type=MESH)
    greet(over)
    greet(twin)
    greet((me, 1 - t))
    greet(twin[:1] + (1 - t,))
    pl.when(has_up)(lambda: greet(up))
    pl.when(has_down)(lambda: greet(down))

    def lanes_of(slot, c):
        return pl.ds(pl.multiple_of((slot * 2 + c) * LANES, LANES), LANES)

    def number(d, r):
        return (z + d) * 2 + (1 - x if r else x)

    def place(shift, d, r, i):
        return all_ref.at[rows_of(chunk(i)), lanes_of(slot_at(z, shift, d, r), core)]

    def along(d, r, i, way):
        q = number(d, r)
        return pltpu.make_async_remote_copy(
            src_ref=place(0, d, r, i), dst_ref=place(1 if way else -1, d, r, i),
            send_sem=z_send.at[way, q, i], recv_sem=recv.at[q, i],
            device_id=(down, up)[way], device_id_type=MESH)

    def across(d, r, i):
        q = number(d, r)
        return pltpu.make_async_remote_copy(
            src_ref=place(0, d, r, i), dst_ref=place(0, d, 1 - r, i),
            send_sem=x_send.at[q, i], recv_sem=recv.at[q, i], device_id=over, device_id_type=MESH)

    def to_twin(d, r, i):
        q = number(d, r)
        return pltpu.make_async_remote_copy(
            src_ref=place(0, d, r, i), dst_ref=place(0, d, r, i), send_sem=c_send.at[q, i],
            recv_sem=c_recv.at[q, i], device_id=twin, device_id_type=MESH)

    def to_panel(d, r, i):
        q, k = number(d, r), chunk(i)
        return pltpu.make_async_remote_copy(
            src_ref=place(0, d, r, i), dst_ref=panel_ref.at[:, lanes_of(slot_at(z, 0, d, r), core)],
            send_sem=y_send.at[q, k % 2], recv_sem=y_recv.at[q * 2 + core],
            device_id=(here * 2 + k % 2, 1 - t), device_id_type=MESH)

    def spread(d, r, i):
        to_twin(d, r, i).start()
        pl.when(owns & (chunk(i) // 2 == part))(lambda: to_panel(d, r, i).start())

    def piece():
        return all_ref.at[pl.ds(0, rows), pl.ds(0, LANES)]

    def landed(sem):
        pltpu.make_async_copy(piece(), piece(), sem).wait()

    def arrive(d, r, i):
        landed(recv.at[number(d, r), i])

    def straight(d):
        crossing = [2 if zz in (0, LINE - 1) else 1 for zz in range(LINE)]
        return pick(z, [count - crossing[zz + d] if 0 <= zz + d < LINE else None for zz in range(LINE)])

    def exists(d):
        return (z + d >= 0) & (z + d < LINE)

    def both_ways(d, r, i):
        pl.when(has_up)(lambda: along(d, r, i, 1).start())
        pl.when(has_down)(lambda: along(d, r, i, 0).start())

    def onward(d, r, i):
        if abs(d) == LINE - 1:
            return
        if d < 0:
            pl.when(has_up)(lambda: along(d, r, i, 1).start())
        else:
            pl.when(has_down)(lambda: along(d, r, i, 0).start())

    def flip(i):
        for copy in inputs(i):
            copy.wait()
        columns = rows_of(chunk(i))
        v = v_buf[:, columns].astype(jnp.float32)
        u = g_buf[:, columns].astype(jnp.float32) * (v / (1.0 + jnp.exp(-v)))
        all_ref[columns, lanes_of(0, core)] = u.astype(jnp.bfloat16).T

    def send_own(i):
        both_ways(0, 0, i)
        across(0, 0, i).start()
        spread(0, 0, i)

    flip(0)
    pl.semaphore_wait(barrier, jnp.where(end, 5, 6))

    @pl.loop(1, count)
    def _(i):
        flip(i)
        send_own(i - 1)

    send_own(count - 1)

    def from_line(d, i):
        @pl.when(exists(d))
        def _():
            arrive(d, 0, i)
            onward(d, 0, i)
            pl.when(i < straight(d))(lambda: across(d, 0, i).start())
            spread(d, 0, i)

    def from_cross(d, i):
        @pl.when(exists(d) & (i >= straight(d)))
        def _():
            arrive(d, 1, i)
            onward(d, 1, i)
            spread(d, 1, i)

    def relayed(d, i):
        @pl.when(exists(d) & (i < straight(d)))
        def _():
            arrive(d, 1, i)
            spread(d, 1, i)

    def neighbour(i):
        arrive(0, 1, i)
        pl.when(i >= straight(0))(lambda: both_ways(0, 1, i))
        spread(0, 1, i)

    def source(slot):
        a = pick(z, [ORDER[zz][slot][0] for zz in range(LINE)])
        r = pick(z, [ORDER[zz][slot][1] for zz in range(LINE)])
        return a * 2 + jnp.where(r == 1, 1 - x, x)

    def complete(slots):
        for slot in slots:
            q = source(slot)

            @pl.loop(0, count)
            def _(i):
                landed(c_recv.at[q, i])

            @pl.when(jnp.logical_not(owns))
            def _():
                for c in range(2):
                    landed(y_recv.at[q * 2 + c])

    def span(slots):
        return pl.ds(slots[0] * 2 * LANES, len(slots) * 2 * LANES)

    def prepare(slots):
        complete(slots)

        @pl.when(owns)
        def _():
            panel_ref[:, span(slots)] = all_ref[rows_of(me % count), span(slots)]

    def multiply(slots, k, add):
        product = nt_dot(all_ref[rows_of(k), span(slots)], panel_ref[:, span(slots)])
        if add:
            product += part_ref[rows_of(k), :]
        part_ref[rows_of(k), :] = product

    @pl.loop(0, count)
    def _(i):
        from_line(-1, i)
        from_line(1, i)
        neighbour(i)

    @pl.loop(0, count)
    def _(i):
        from_line(-2, i)
        from_line(2, i)
        from_cross(-1, i)
        from_cross(1, i)

        @pl.when(end)
        def _():
            relayed(-1, i)
            relayed(1, i)

        @pl.when(jnp.logical_not(end))
        def _():
            pl.when(i % 2 == 0)(lambda: relayed(-1, i // 2))
            pl.when(i % 2 == 1)(lambda: relayed(1, i // 2))

    prepare(FIRST)

    @pl.loop(0, count)
    def _(i):
        multiply(FIRST, i, False)
        from_line(-3, i)
        from_line(3, i)
        from_cross(-2, i)
        from_cross(2, i)

        @pl.when(end)
        def _():
            relayed(-2, i)
            relayed(2, i)

        @pl.when(jnp.logical_not(end))
        def _():
            later = (count + i) // 2
            pl.when(i % 2 == 0)(lambda: relayed(-1, later))
            pl.when(i % 2 == 1)(lambda: relayed(1, later))

    prepare(SECOND)

    @pl.loop(0, count)
    def _(i):
        multiply(SECOND, i, True)
        from_cross(-3, i)
        from_cross(3, i)

        @pl.when(end)
        def _():
            relayed(-3, i)
            relayed(3, i)

        @pl.when(jnp.logical_not(end))
        def _():
            relayed(-2, i)
            relayed(2, i)

    complete([LAST])

    @pl.loop(0, CHIPS)
    def _(q):
        away, mine = q // 2, q % 2 == x
        crossing = jnp.where((away == 0) | (away == LINE - 1), 2, 1)

        @pl.loop(0, count)
        def _(i):
            landed(c_send.at[q, i])
            pl.when(mine & ((i < count - crossing) | (away == z)))(lambda: landed(x_send.at[q, i]))
            goes = mine | (i >= count - crossing)
            pl.when(goes & has_up & (away <= z))(lambda: landed(z_send.at[1, q, i]))
            pl.when(goes & has_down & (away >= z))(lambda: landed(z_send.at[0, q, i]))

        @pl.when(owns)
        def _():
            for j in range(2):
                landed(y_send.at[q, j])


def gather(grad_hidden, gate, width, tokens):
    mine, hidden = gate.shape
    count = hidden // width
    sem = pltpu.SemaphoreType.DMA
    vmem = pl.BlockSpec(memory_space=pltpu.VMEM)
    held = hidden * tokens * 2 + width * tokens * 2 + hidden * width * 4
    return pl.pallas_call(
        functools.partial(gather_kernel, (count, width)),
        out_shape=(
            pltpu.VMEM((hidden, tokens), jnp.bfloat16),
            pltpu.VMEM((width, tokens), jnp.bfloat16),
            pltpu.VMEM((hidden, width), jnp.float32),
        ),
        in_specs=[pl.BlockSpec(memory_space=pl.ANY)] * 2,
        out_specs=(vmem, vmem, vmem),
        scratch_shapes=[
            pltpu.VMEM((mine, hidden), jnp.bfloat16),
            pltpu.VMEM((mine, hidden), jnp.bfloat16),
            sem((count,)),
            sem((count,)),
            sem((2, CHIPS, count)),
            sem((CHIPS, count)),
            sem((CHIPS, count)),
            sem((CHIPS, 2)),
            sem((CHIPS, count)),
            sem((CHIPS, count)),
            sem((2 * CHIPS,)),
        ],
        compiler_params=pltpu.CompilerParams(
            collective_id=0, has_side_effects=True, vmem_limit_bytes=VMEM_BYTES - held - 2**18
        ),
    )(grad_hidden, gate)


def finish_kernel(total, tile, depth, all_ref, panel_ref, part_ref, o_ref, b_ref, o_buf, sem):
    me, t, z, x, core = position()
    width = panel_ref.shape[0]
    count = all_ref.shape[0] // width
    lanes = pl.ds(LAST * 2 * LANES, 2 * LANES)

    for ours in (True, False):
        @pl.when((me // count == t) == ours)
        def _():
            rows = pl.ds(pl.multiple_of(me % count * width, width), width)
            b_ref[...] = all_ref[rows, lanes] if ours else panel_ref[:, lanes]

    def rows_of(i):
        return pl.ds(pl.multiple_of(i * tile, tile), tile)

    def out(i):
        slot = i % depth
        return pltpu.make_async_copy(o_buf.at[slot], o_ref.at[rows_of(i)], sem.at[slot])

    steps = o_ref.shape[0] // tile

    @pl.loop(0, steps)
    def _(i):
        pl.when(i >= depth)(lambda: out(i - depth).wait())
        product = nt_dot(all_ref[rows_of(i), lanes], b_ref[...])
        o_buf[i % depth] = (part_ref[rows_of(i), :] + product) * (1.0 / total)
        out(i).start()

    @pl.loop(steps - depth, steps)
    def _(i):
        out(i).wait()


def finish(everything, panel, part, tile, depth):
    hidden, tokens = everything.shape
    width = panel.shape[0]
    held = hidden * tokens * 2 + width * tokens * 2 + hidden * width * 4
    keep = lambda array: pltpu.with_memory_space_constraint(array, pltpu.VMEM)
    return pl.pallas_call(
        functools.partial(finish_kernel, tokens, tile, depth),
        out_shape=jax.ShapeDtypeStruct((hidden, width), jnp.float32),
        in_specs=[pl.BlockSpec(memory_space=pltpu.VMEM)] * 3,
        out_specs=pl.BlockSpec(memory_space=pl.ANY),
        scratch_shapes=[
            pltpu.VMEM((width, 2 * LANES), jnp.bfloat16),
            pltpu.VMEM((depth, tile, width), jnp.float32),
            pltpu.SemaphoreType.DMA((depth,)),
        ],
        compiler_params=pltpu.CompilerParams(vmem_limit_bytes=VMEM_BYTES - held - 2**18),
    )(keep(everything), keep(panel), keep(part))


def shards(grad_hidden, gate):
    tensor_count, data_count = lax.axis_size("tensor"), lax.axis_size("dp")
    mine, hidden = grad_hidden.shape
    width = hidden * tensor_count // data_count
    tokens = mine * data_count
    held = hidden * tokens * 2 + width * tokens * 2 + hidden * width * 4
    fits = (
        tensor_count == 2 and data_count == 4 * LINE and mine == LANES and width % LANES == 0
        and tokens & (tokens - 1) == 0 and held + 7 * 2**20 < VMEM_BYTES
    )
    if not fits:
        return plain(grad_hidden, gate)
    everything, panel, part = gather(grad_hidden, gate, width, tokens)
    return finish(everything, panel, part, width // 2, 3)


def solution(mesh):
    return jax.shard_map(
        shards,
        mesh=mesh,
        in_specs=(P("dp", "tensor"), P("dp", "tensor")),
        out_specs=P("tensor", "dp"),
        check_vma=False,
    )
```

time: 197 us -> 163 us (0.83)
  the two profiles are of different devices: /device:TPU:27 before, /device:TPU:7 now
where the time goes in v1:
time: 163 us
  Pallas kernels  163 us (100%)
    pallas_call x1, Pallas kernels, gather(): pl.pallas_call(functools.partial(gather_kernel, (count, width)), out_shap...  153 us
    pallas_call x1, Pallas kernels, finish(): pl.pallas_call(functools.partial(finish_kernel, tokens, tile, depth), out...  9.65 us

profile of v1, /device:TPU:7, one launch (start us, length us, event | category | flops | bytes accessed | tf_op | source)
XLA Modules:
  0.0 163.1 jit_solution(6626023715112197561)
XLA Ops:
  0.0 153.4 %shard_map.28 = (bf16[7168,2048]{1,0:T(8,128)(2,1)S(1)}, bf16[896,2048]{1,0:T(8,128)(2,1)S(1)}, f32[7168,896]{1,0:T(8,128)S(1)}) custom-call(bf16[128,7168]{1,0:T(8,128)(2,1)} %g_ref.1, bf16[128,7168]{1,0:T(8,128)(2,1)} %v_ref.1), custom_call_target="tpu_custom_call" | custom-call | tf_op jit(solution)/shard_map/pallas_call | solution.py:362
  153.4 9.6 %shard_map.29 = f32[7168,896]{1,0:T(8,128)} custom-call(bf16[7168,2048]{1,0:T(8,128)(2,1)S(1)} %get-tuple-element.8.all_ref, bf16[896,2048]{1,0:T(8,128)(2,1)S(1)} %get-tuple-element.9.panel_ref, f32[7168,896]{1,0:T(8,128)S(1)} %get-tuple-element.10.part_ref), custom_call_target="tpu_custom_call" | custom-call | tf_op jit(solution)/shard_map/pallas_call | solution.py:428

commit v2 on v1

--- a/solution.py
+++ b/solution.py
@@ -83,6 +83,7 @@
     me, t, z, x, core = position()
     here = me // 2
     half = CHIPS // 2
+    early = count // 2
     owns = here // half == t
     part = here % half
     end = (z == 0) | (z == LINE - 1)
@@ -100,16 +101,13 @@
         return pl.ds(pl.multiple_of(k * rows, rows), rows)
 
     def inputs(i):
-        columns = rows_of(chunk(i))
         return [
-            pltpu.make_async_copy(src.at[:, columns], dst.at[:, columns], sem.at[i])
+            pltpu.make_async_copy(src.at[:, rows_of(chunk(i))], dst.at[i % 2], sem.at[i % 2])
             for src, dst, sem in ((g_ref, g_buf, g_sem), (v_ref, v_buf, v_sem))
         ]
 
-    @pl.loop(0, count)
-    def _(i):
-        for copy in inputs(i):
-            copy.start()
+    for copy in inputs(0):
+        copy.start()
 
     barrier = pltpu.get_barrier_semaphore()
     greet = lambda dev: pl.semaphore_signal(barrier, inc=1, device_id=dev, device_id_type=MESH)
@@ -191,8 +189,8 @@
         for copy in inputs(i):
             copy.wait()
         columns = rows_of(chunk(i))
-        v = v_buf[:, columns].astype(jnp.float32)
-        u = g_buf[:, columns].astype(jnp.float32) * (v / (1.0 + jnp.exp(-v)))
+        v = v_buf[i % 2].astype(jnp.float32)
+        u = g_buf[i % 2].astype(jnp.float32) * (v / (1.0 + jnp.exp(-v)))
         all_ref[columns, lanes_of(0, core)] = u.astype(jnp.bfloat16).T
 
     def send_own(i):
@@ -200,11 +198,20 @@
         across(0, 0, i).start()
         spread(0, 0, i)
 
+    def fetch(i):
+        for copy in inputs(i):
+            copy.start()
+
     flip(0)
+    fetch(1)
     pl.semaphore_wait(barrier, jnp.where(end, 5, 6))
-
-    @pl.loop(1, count)
-    def _(i):
+    send_own(0)
+    fetch(2)
+    flip(1)
+
+    @pl.loop(2, count)
+    def _(i):
+        pl.when(i + 1 < count)(lambda: fetch(i + 1))
         flip(i)
         send_own(i - 1)
 
@@ -241,24 +248,25 @@
         r = pick(z, [ORDER[zz][slot][1] for zz in range(LINE)])
         return a * 2 + jnp.where(r == 1, 1 - x, x)
 
-    def complete(slots):
-        for slot in slots:
-            q = source(slot)
-
-            @pl.loop(0, count)
-            def _(i):
-                landed(c_recv.at[q, i])
-
-            @pl.when(jnp.logical_not(owns))
-            def _():
-                for c in range(2):
-                    landed(y_recv.at[q * 2 + c])
-
     def span(slots):
         return pl.ds(slots[0] * 2 * LANES, len(slots) * 2 * LANES)
 
-    def prepare(slots):
-        complete(slots)
+    def twin_sent(slots, i):
+        for slot in slots:
+            landed(c_recv.at[source(slot), i])
+
+    def all_twin_sent(slots, first, last):
+        @pl.loop(first, last)
+        def _(i):
+            twin_sent(slots, i)
+
+    def panel_arrived(slots):
+        for slot in slots:
+            for c in range(2):
+                landed(y_recv.at[source(slot) * 2 + c])
+
+    def columns(slots):
+        pl.when(jnp.logical_not(owns))(lambda: panel_arrived(slots))
 
         @pl.when(owns)
         def _():
@@ -293,11 +301,12 @@
             pl.when(i % 2 == 0)(lambda: relayed(-1, i // 2))
             pl.when(i % 2 == 1)(lambda: relayed(1, i // 2))
 
-    prepare(FIRST)
+    all_twin_sent(FIRST, 0, count)
+    columns(FIRST)
 
     @pl.loop(0, count)
     def _(i):
-        multiply(FIRST, i, False)
+        multiply(FIRST, chunk(i), False)
         from_line(-3, i)
         from_line(3, i)
         from_cross(-2, i)
@@ -314,11 +323,43 @@
             pl.when(i % 2 == 0)(lambda: relayed(-1, later))
             pl.when(i % 2 == 1)(lambda: relayed(1, later))
 
-    prepare(SECOND)
+        @pl.when(end & (i == early))
+        def _():
+            all_twin_sent(SECOND, 0, early)
+            columns(SECOND)
+
+        @pl.when(end & (i >= early))
+        def _():
+            multiply(SECOND, chunk(i - early), True)
+
+    @pl.when(jnp.logical_not(end))
+    def _():
+        all_twin_sent(SECOND, 0, count)
+        columns(SECOND)
+
+    def sent(nearby):
+        @pl.loop(0, CHIPS)
+        def _(q):
+            away, mine = q // 2, q % 2 == x
+            crossing = jnp.where((away == 0) | (away == LINE - 1), 2, 1)
+
+            @pl.when((jnp.abs(away - z) <= 1) == nearby)
+            def _():
+                @pl.loop(0, count)
+                def _(i):
+                    landed(c_send.at[q, i])
+                    pl.when(mine & ((i < count - crossing) | (away == z)))(lambda: landed(x_send.at[q, i]))
+                    goes = mine | (i >= count - crossing)
+                    pl.when(goes & has_up & (away <= z))(lambda: landed(z_send.at[1, q, i]))
+                    pl.when(goes & has_down & (away >= z))(lambda: landed(z_send.at[0, q, i]))
+
+                @pl.when(owns)
+                def _():
+                    for j in range(2):
+                        landed(y_send.at[q, j])
 
     @pl.loop(0, count)
     def _(i):
-        multiply(SECOND, i, True)
         from_cross(-3, i)
         from_cross(3, i)
 
@@ -332,25 +373,18 @@
             relayed(-2, i)
             relayed(2, i)
 
-    complete([LAST])
-
-    @pl.loop(0, CHIPS)
-    def _(q):
-        away, mine = q // 2, q % 2 == x
-        crossing = jnp.where((away == 0) | (away == LINE - 1), 2, 1)
-
-        @pl.loop(0, count)
-        def _(i):
-            landed(c_send.at[q, i])
-            pl.when(mine & ((i < count - crossing) | (away == z)))(lambda: landed(x_send.at[q, i]))
-            goes = mine | (i >= count - crossing)
-            pl.when(goes & has_up & (away <= z))(lambda: landed(z_send.at[1, q, i]))
-            pl.when(goes & has_down & (away >= z))(lambda: landed(z_send.at[0, q, i]))
-
-        @pl.when(owns)
-        def _():
-            for j in range(2):
-                landed(y_send.at[q, j])
+        later = jnp.where(end, i + count - early, i)
+
+        @pl.when(later < count)
+        def _():
+            pl.when(end)(lambda: twin_sent(SECOND, later))
+            multiply(SECOND, chunk(later), True)
+
+        pl.when(i == early)(lambda: sent(True))
+
+    all_twin_sent([LAST], 0, count)
+    pl.when(jnp.logical_not(owns))(lambda: panel_arrived([LAST]))
+    sent(False)
 
 
 def gather(grad_hidden, gate, width, tokens):
@@ -369,10 +403,10 @@
         in_specs=[pl.BlockSpec(memory_space=pl.ANY)] * 2,
         out_specs=(vmem, vmem, vmem),
         scratch_shapes=[
-            pltpu.VMEM((mine, hidden), jnp.bfloat16),
-            pltpu.VMEM((mine, hidden), jnp.bfloat16),
-            sem((count,)),
-            sem((count,)),
+            pltpu.VMEM((2, mine, width), jnp.bfloat16),
+            pltpu.VMEM((2, mine, width), jnp.bfloat16),
+            sem((2,)),
+            sem((2,)),
             sem((2, CHIPS, count)),
             sem((CHIPS, count)),
             sem((CHIPS, count)),
@@ -387,7 +421,7 @@
     )(grad_hidden, gate)
 
 
-def finish_kernel(total, tile, depth, all_ref, panel_ref, part_ref, o_ref, b_ref, o_buf, sem):
+def finish_kernel(total, tile, all_ref, panel_ref, _, o_ref, part_ref, b_ref, sem):
     me, t, z, x, core = position()
     width = panel_ref.shape[0]
     count = all_ref.shape[0] // width
@@ -403,40 +437,42 @@
         return pl.ds(pl.multiple_of(i * tile, tile), tile)
 
     def out(i):
-        slot = i % depth
-        return pltpu.make_async_copy(o_buf.at[slot], o_ref.at[rows_of(i)], sem.at[slot])
+        return pltpu.make_async_copy(part_ref.at[rows_of(i)], o_ref.at[rows_of(i)], sem.at[i])
 
     steps = o_ref.shape[0] // tile
 
     @pl.loop(0, steps)
     def _(i):
-        pl.when(i >= depth)(lambda: out(i - depth).wait())
         product = nt_dot(all_ref[rows_of(i), lanes], b_ref[...])
-        o_buf[i % depth] = (part_ref[rows_of(i), :] + product) * (1.0 / total)
+        part_ref[rows_of(i), :] = (part_ref[rows_of(i), :] + product) * (1.0 / total)
         out(i).start()
 
-    @pl.loop(steps - depth, steps)
+    @pl.loop(0, steps)
     def _(i):
         out(i).wait()
 
 
-def finish(everything, panel, part, tile, depth):
+def finish(everything, panel, part, tile):
     hidden, tokens = everything.shape
     width = panel.shape[0]
     held = hidden * tokens * 2 + width * tokens * 2 + hidden * width * 4
     keep = lambda array: pltpu.with_memory_space_constraint(array, pltpu.VMEM)
+    vmem = pl.BlockSpec(memory_space=pltpu.VMEM)
     return pl.pallas_call(
-        functools.partial(finish_kernel, tokens, tile, depth),
-        out_shape=jax.ShapeDtypeStruct((hidden, width), jnp.float32),
-        in_specs=[pl.BlockSpec(memory_space=pltpu.VMEM)] * 3,
-        out_specs=pl.BlockSpec(memory_space=pl.ANY),
+        functools.partial(finish_kernel, tokens, tile),
+        out_shape=(
+            jax.ShapeDtypeStruct((hidden, width), jnp.float32),
+            pltpu.VMEM((hidden, width), jnp.float32),
+        ),
+        in_specs=[vmem] * 3,
+        out_specs=(pl.BlockSpec(memory_space=pl.ANY), vmem),
+        input_output_aliases={2: 1},
         scratch_shapes=[
             pltpu.VMEM((width, 2 * LANES), jnp.bfloat16),
-            pltpu.VMEM((depth, tile, width), jnp.float32),
-            pltpu.SemaphoreType.DMA((depth,)),
+            pltpu.SemaphoreType.DMA((hidden // tile,)),
         ],
         compiler_params=pltpu.CompilerParams(vmem_limit_bytes=VMEM_BYTES - held - 2**18),
-    )(keep(everything), keep(panel), keep(part))
+    )(keep(everything), keep(panel), keep(part))[0]
 
 
 def shards(grad_hidden, gate):
@@ -452,7 +488,7 @@
     if not fits:
         return plain(grad_hidden, gate)
     everything, panel, part = gather(grad_hidden, gate, width, tokens)
-    return finish(everything, panel, part, width // 2, 3)
+    return finish(everything, panel, part, width // 2)
 
 
 def solution(mesh):

time: 163 us -> 160 us (0.982)
  Pallas kernels: 163 us -> 160 us
    pallas_call x1, Pallas kernels: 153 us -> 150 us  [gather(): pl.pallas_call(functools.partial(gather_kernel, (count, width)), out_shap...]
where the time goes in v2:
time: 160 us
  Pallas kernels  160 us (100%)
    pallas_call x1, Pallas kernels, gather(): pl.pallas_call(functools.partial(gather_kernel, (count, width)), out_shap...  150 us
    pallas_call x1, Pallas kernels, finish(): pl.pallas_call(functools.partial(finish_kernel, tokens, tile), out_shape=...  9.19 us

profile of v2, /device:TPU:7, one launch (start us, length us, event | category | flops | bytes accessed | tf_op | source)
XLA Modules:
  0.0 159.7 jit_solution(1152840146919197922)
XLA Ops:
  0.0 150.5 %shard_map.28 = (bf16[7168,2048]{1,0:T(8,128)(2,1)S(1)}, bf16[896,2048]{1,0:T(8,128)(2,1)S(1)}, f32[7168,896]{1,0:T(8,128)S(1)}) custom-call(bf16[128,7168]{1,0:T(8,128)(2,1)} %g_ref.1, bf16[128,7168]{1,0:T(8,128)(2,1)} %v_ref.1), custom_call_target="tpu_custom_call" | custom-call | tf_op jit(solution)/shard_map/pallas_call | solution.py:396
  150.5 9.2 %shard_map.29 = (f32[7168,896]{1,0:T(8,128)}, f32[7168,896]{1,0:T(8,128)S(1)}) custom-call(bf16[7168,2048]{1,0:T(8,128)(2,1)S(1)} %get-tuple-element.9.all_ref, bf16[896,2048]{1,0:T(8,128)(2,1)S(1)} %get-tuple-element.10.panel_ref, f32[7168,896]{1,0:T(8,128)S(1)} %get-tuple-element.11._), custom_call_target="tpu_custom_call", output_to_operand_aliasing={{1}: (2, {})} | custom-call | tf_op jit(solution)/shard_map/pallas_call | solution.py:461

commit v3 on v2

--- a/solution.py
+++ b/solution.py
@@ -20,6 +20,7 @@
 ORDER = [BOTTOM[z] if z in BOTTOM else [(LINE - 1 - a, r) for a, r in BOTTOM[LINE - 1 - z]] for z in range(LINE)]
 FIRST, SECOND = range(0, 5), range(5, 7)
 LAST = CHIPS - 1
+CROSSING = [2 if z in (0, LINE - 1) else 1 for z in range(LINE)]
 
 
 def activations(grad_hidden, gate):
@@ -131,44 +132,44 @@
         q = number(d, r)
         return pltpu.make_async_remote_copy(
             src_ref=place(0, d, r, i), dst_ref=place(1 if way else -1, d, r, i),
-            send_sem=z_send.at[way, q, i], recv_sem=recv.at[q, i],
+            send_sem=z_send.at[way], recv_sem=recv.at[q, i],
             device_id=(down, up)[way], device_id_type=MESH)
 
     def across(d, r, i):
         q = number(d, r)
         return pltpu.make_async_remote_copy(
             src_ref=place(0, d, r, i), dst_ref=place(0, d, 1 - r, i),
-            send_sem=x_send.at[q, i], recv_sem=recv.at[q, i], device_id=over, device_id_type=MESH)
+            send_sem=x_send, recv_sem=recv.at[q, i], device_id=over, device_id_type=MESH)
 
     def to_twin(d, r, i):
-        q = number(d, r)
+        slot = slot_at(z, 0, d, r)
+        later = 2 + jnp.maximum(i - early + 1, 0)
+        index = jnp.where(slot < SECOND[0], 0, jnp.where(slot == LAST, 1, later))
         return pltpu.make_async_remote_copy(
-            src_ref=place(0, d, r, i), dst_ref=place(0, d, r, i), send_sem=c_send.at[q, i],
-            recv_sem=c_recv.at[q, i], device_id=twin, device_id_type=MESH)
+            src_ref=place(0, d, r, i), dst_ref=place(0, d, r, i), send_sem=c_send,
+            recv_sem=c_recv.at[index], device_id=twin, device_id_type=MESH)
 
     def to_panel(d, r, i):
-        q, k = number(d, r), chunk(i)
+        k, slot = chunk(i), slot_at(z, 0, d, r)
+        index = jnp.where(slot < SECOND[0], 0, jnp.where(slot == LAST, 2, 1))
         return pltpu.make_async_remote_copy(
-            src_ref=place(0, d, r, i), dst_ref=panel_ref.at[:, lanes_of(slot_at(z, 0, d, r), core)],
-            send_sem=y_send.at[q, k % 2], recv_sem=y_recv.at[q * 2 + core],
+            src_ref=place(0, d, r, i), dst_ref=panel_ref.at[:, lanes_of(slot, core)],
+            send_sem=y_send, recv_sem=y_recv.at[index],
             device_id=(here * 2 + k % 2, 1 - t), device_id_type=MESH)
 
     def spread(d, r, i):
         to_twin(d, r, i).start()
         pl.when(owns & (chunk(i) // 2 == part))(lambda: to_panel(d, r, i).start())
 
-    def piece():
-        return all_ref.at[pl.ds(0, rows), pl.ds(0, LANES)]
-
-    def landed(sem):
-        pltpu.make_async_copy(piece(), piece(), sem).wait()
+    def landed(sem, chunks=1):
+        piece = all_ref.at[pl.ds(0, chunks * rows // 8), pl.ds(0, 8 * LANES)]
+        pltpu.make_async_copy(piece, piece, sem).wait()
 
     def arrive(d, r, i):
         landed(recv.at[number(d, r), i])
 
     def straight(d):
-        crossing = [2 if zz in (0, LINE - 1) else 1 for zz in range(LINE)]
-        return pick(z, [count - crossing[zz + d] if 0 <= zz + d < LINE else None for zz in range(LINE)])
+        return pick(z, [count - CROSSING[zz + d] if 0 <= zz + d < LINE else None for zz in range(LINE)])
 
     def exists(d):
         return (z + d >= 0) & (z + d < LINE)
@@ -243,30 +244,11 @@
         pl.when(i >= straight(0))(lambda: both_ways(0, 1, i))
         spread(0, 1, i)
 
-    def source(slot):
-        a = pick(z, [ORDER[zz][slot][0] for zz in range(LINE)])
-        r = pick(z, [ORDER[zz][slot][1] for zz in range(LINE)])
-        return a * 2 + jnp.where(r == 1, 1 - x, x)
-
     def span(slots):
         return pl.ds(slots[0] * 2 * LANES, len(slots) * 2 * LANES)
 
-    def twin_sent(slots, i):
-        for slot in slots:
-            landed(c_recv.at[source(slot), i])
-
-    def all_twin_sent(slots, first, last):
-        @pl.loop(first, last)
-        def _(i):
-            twin_sent(slots, i)
-
-    def panel_arrived(slots):
-        for slot in slots:
-            for c in range(2):
-                landed(y_recv.at[source(slot) * 2 + c])
-
-    def columns(slots):
-        pl.when(jnp.logical_not(owns))(lambda: panel_arrived(slots))
+    def columns(slots, group):
+        pl.when(jnp.logical_not(owns))(lambda: landed(y_recv.at[group], 2 * len(slots)))
 
         @pl.when(owns)
         def _():
@@ -301,8 +283,8 @@
             pl.when(i % 2 == 0)(lambda: relayed(-1, i // 2))
             pl.when(i % 2 == 1)(lambda: relayed(1, i // 2))
 
-    all_twin_sent(FIRST, 0, count)
-    columns(FIRST)
+    landed(c_recv.at[0], len(FIRST) * count)
+    columns(FIRST, 0)
 
     @pl.loop(0, count)
     def _(i):
@@ -325,8 +307,8 @@
 
         @pl.when(end & (i == early))
         def _():
-            all_twin_sent(SECOND, 0, early)
-            columns(SECOND)
+            landed(c_recv.at[2], len(SECOND) * early)
+            columns(SECOND, 1)
 
         @pl.when(end & (i >= early))
         def _():
@@ -334,29 +316,10 @@
 
     @pl.when(jnp.logical_not(end))
     def _():
-        all_twin_sent(SECOND, 0, count)
-        columns(SECOND)
-
-    def sent(nearby):
-        @pl.loop(0, CHIPS)
-        def _(q):
-            away, mine = q // 2, q % 2 == x
-            crossing = jnp.where((away == 0) | (away == LINE - 1), 2, 1)
-
-            @pl.when((jnp.abs(away - z) <= 1) == nearby)
-            def _():
-                @pl.loop(0, count)
-                def _(i):
-                    landed(c_send.at[q, i])
-                    pl.when(mine & ((i < count - crossing) | (away == z)))(lambda: landed(x_send.at[q, i]))
-                    goes = mine | (i >= count - crossing)
-                    pl.when(goes & has_up & (away <= z))(lambda: landed(z_send.at[1, q, i]))
-                    pl.when(goes & has_down & (away >= z))(lambda: landed(z_send.at[0, q, i]))
-
-                @pl.when(owns)
-                def _():
-                    for j in range(2):
-                        landed(y_send.at[q, j])
+        landed(c_recv.at[2], len(SECOND) * early)
+        for i in range(early, count):
+            landed(c_recv.at[3 + i - early], len(SECOND))
+        columns(SECOND, 1)
 
     @pl.loop(0, count)
     def _(i):
@@ -377,14 +340,21 @@
 
         @pl.when(later < count)
         def _():
-            pl.when(end)(lambda: twin_sent(SECOND, later))
+            pl.when(end)(lambda: landed(c_recv.at[3 + i], len(SECOND)))
             multiply(SECOND, chunk(later), True)
 
-        pl.when(i == early)(lambda: sent(True))
-
-    all_twin_sent([LAST], 0, count)
-    pl.when(jnp.logical_not(owns))(lambda: panel_arrived([LAST]))
-    sent(False)
+    landed(c_recv.at[1], count)
+    pl.when(jnp.logical_not(owns))(lambda: landed(y_recv.at[2], 2))
+    landed(c_send, CHIPS * count)
+    pl.when(owns)(lambda: landed(y_send, 2 * CHIPS))
+    for zz in range(LINE):
+        @pl.when(z == zz)
+        def _():
+            landed(x_send, CROSSING[zz] + sum(count - c for c in CROSSING))
+            if zz < LINE - 1:
+                landed(z_send.at[1], sum(count + c for c in CROSSING[:zz + 1]))
+            if zz > 0:
+                landed(z_send.at[0], sum(count + c for c in CROSSING[zz:]))
 
 
 def gather(grad_hidden, gate, width, tokens):
@@ -407,13 +377,13 @@
             pltpu.VMEM((2, mine, width), jnp.bfloat16),
             sem((2,)),
             sem((2,)),
-            sem((2, CHIPS, count)),
+            sem((2,)),
+            sem(()),
+            sem(()),
+            sem(()),
             sem((CHIPS, count)),
-            sem((CHIPS, count)),
-            sem((CHIPS, 2)),
-            sem((CHIPS, count)),
-            sem((CHIPS, count)),
-            sem((2 * CHIPS,)),
+            sem((3 + count - count // 2,)),
+            sem((3,)),
         ],
         compiler_params=pltpu.CompilerParams(
             collective_id=0, has_side_effects=True, vmem_limit_bytes=VMEM_BYTES - held - 2**18

time: 160 us -> 156 us (0.975)
  Pallas kernels: 160 us -> 156 us
    pallas_call x1, Pallas kernels: 150 us -> 147 us  [gather(): pl.pallas_call(functools.partial(gather_kernel, (count, width)), out_shap...]
where the time goes in v3:
time: 156 us
  Pallas kernels  156 us (100%)
    pallas_call x1, Pallas kernels, gather(): pl.pallas_call(functools.partial(gather_kernel, (count, width)), out_shap...  147 us
    pallas_call x1, Pallas kernels, finish(): pl.pallas_call(functools.partial(finish_kernel, tokens, tile), out_shape=...  9.19 us

profile of v3, /device:TPU:7, one launch (start us, length us, event | category | flops | bytes accessed | tf_op | source)
XLA Modules:
  0.0 156.1 jit_solution(12893579818431949018)
XLA Ops:
  0.0 146.9 %shard_map.28 = (bf16[7168,2048]{1,0:T(8,128)(2,1)S(1)}, bf16[896,2048]{1,0:T(8,128)(2,1)S(1)}, f32[7168,896]{1,0:T(8,128)S(1)}) custom-call(bf16[128,7168]{1,0:T(8,128)(2,1)} %g_ref.1, bf16[128,7168]{1,0:T(8,128)(2,1)} %v_ref.1), custom_call_target="tpu_custom_call" | custom-call | tf_op jit(solution)/shard_map/pallas_call | solution.py:366
  146.9 9.2 %shard_map.29 = (f32[7168,896]{1,0:T(8,128)}, f32[7168,896]{1,0:T(8,128)S(1)}) custom-call(bf16[7168,2048]{1,0:T(8,128)(2,1)S(1)} %get-tuple-element.9.all_ref, bf16[896,2048]{1,0:T(8,128)(2,1)S(1)} %get-tuple-element.10.panel_ref, f32[7168,896]{1,0:T(8,128)S(1)} %get-tuple-element.11._), custom_call_target="tpu_custom_call", output_to_operand_aliasing={{1}: (2, {})} | custom-call | tf_op jit(solution)/shard_map/pallas_call | solution.py:431

commit v4 on v3

--- a/solution.py
+++ b/solution.py
@@ -305,6 +305,11 @@
             pl.when(i % 2 == 0)(lambda: relayed(-1, later))
             pl.when(i % 2 == 1)(lambda: relayed(1, later))
 
+        @pl.when(end & (i > early))
+        def _():
+            relayed(-3, i - early - 1)
+            relayed(3, i - early - 1)
+
         @pl.when(end & (i == early))
         def _():
             landed(c_recv.at[2], len(SECOND) * early)
@@ -321,15 +326,19 @@
             landed(c_recv.at[3 + i - early], len(SECOND))
         columns(SECOND, 1)
 
+    ahead = count - early - 1
+
     @pl.loop(0, count)
     def _(i):
-        from_cross(-3, i)
-        from_cross(3, i)
-
-        @pl.when(end)
-        def _():
-            relayed(-3, i)
-            relayed(3, i)
+        @pl.when(end & (i % 2 == 0))
+        def _():
+            relayed(-3, ahead + i // 2)
+            relayed(3, ahead + i // 2)
+
+        @pl.when(end & ((i == 2) | (i == 4)))
+        def _():
+            from_cross(-3, count - 3 + i // 2)
+            from_cross(3, count - 3 + i // 2)
 
         @pl.when(jnp.logical_not(end))
         def _():

time: 156 us -> 155 us (level); the launches traced: 156 us -> 153 us
  Pallas kernels: 156 us -> 153 us
    pallas_call x1, Pallas kernels: 147 us -> 144 us  [gather(): pl.pallas_call(functools.partial(gather_kernel, (count, width)), out_shap...]
where the time goes in v4:
time: 155 us; the launch traced here: 153 us
  Pallas kernels  153 us (99%)
    pallas_call x1, Pallas kernels, gather(): pl.pallas_call(functools.partial(gather_kernel, (count, width)), out_shap...  144 us
    pallas_call x1, Pallas kernels, finish(): pl.pallas_call(functools.partial(finish_kernel, tokens, tile), out_shape=...  9.19 us

profile of v4, /device:TPU:7, one launch (start us, length us, event | category | flops | bytes accessed | tf_op | source)
XLA Modules:
  0.0 152.8 jit_solution(14959728119121877999)
XLA Ops:
  0.0 143.6 %shard_map.28 = (bf16[7168,2048]{1,0:T(8,128)(2,1)S(1)}, bf16[896,2048]{1,0:T(8,128)(2,1)S(1)}, f32[7168,896]{1,0:T(8,128)S(1)}) custom-call(bf16[128,7168]{1,0:T(8,128)(2,1)} %g_ref.1, bf16[128,7168]{1,0:T(8,128)(2,1)} %v_ref.1), custom_call_target="tpu_custom_call" | custom-call | tf_op jit(solution)/shard_map/pallas_call | solution.py:375
  143.6 9.2 %shard_map.29 = (f32[7168,896]{1,0:T(8,128)}, f32[7168,896]{1,0:T(8,128)S(1)}) custom-call(bf16[7168,2048]{1,0:T(8,128)(2,1)S(1)} %get-tuple-element.9.all_ref, bf16[896,2048]{1,0:T(8,128)(2,1)S(1)} %get-tuple-element.10.panel_ref, f32[7168,896]{1,0:T(8,128)S(1)} %get-tuple-element.11._), custom_call_target="tpu_custom_call", output_to_operand_aliasing={{1}: (2, {})} | custom-call | tf_op jit(solution)/shard_map/pallas_call | solution.py:440

commit v5 on v4

--- a/solution.py
+++ b/solution.py
@@ -20,6 +20,7 @@
 ORDER = [BOTTOM[z] if z in BOTTOM else [(LINE - 1 - a, r) for a, r in BOTTOM[LINE - 1 - z]] for z in range(LINE)]
 FIRST, SECOND = range(0, 5), range(5, 7)
 LAST = CHIPS - 1
+READY = 2
 CROSSING = [2 if z in (0, LINE - 1) else 1 for z in range(LINE)]
 
 
@@ -78,9 +79,9 @@
 
 def gather_kernel(
     dims, g_ref, v_ref, all_ref, panel_ref, part_ref, g_buf, v_buf, g_sem, v_sem,
-    z_send, x_send, c_send, y_send, recv, c_recv, y_recv,
+    z_send, x_send, c_send, y_send, recv, tail, c_recv, y_recv,
 ):
-    count, rows = dims
+    count, rows, total = dims
     me, t, z, x, core = position()
     here = me // 2
     half = CHIPS // 2
@@ -125,28 +126,31 @@
     def number(d, r):
         return (z + d) * 2 + (1 - x if r else x)
 
-    def place(shift, d, r, i):
-        return all_ref.at[rows_of(chunk(i)), lanes_of(slot_at(z, shift, d, r), core)]
-
-    def along(d, r, i, way):
-        q = number(d, r)
+    def place(shift, d, r, i, h=None):
+        k, lanes = chunk(i), lanes_of(slot_at(z, shift, d, r), core)
+        if h is None:
+            return all_ref.at[rows_of(k), lanes]
+        return all_ref.at[pl.ds(pl.multiple_of(k * rows + h * (rows // 2), rows // 2), rows // 2), lanes]
+
+    def along(d, r, i, way, h=None):
         return pltpu.make_async_remote_copy(
-            src_ref=place(0, d, r, i), dst_ref=place(1 if way else -1, d, r, i),
-            send_sem=z_send.at[way], recv_sem=recv.at[q, i],
+            src_ref=place(0, d, r, i, h), dst_ref=place(1 if way else -1, d, r, i, h),
+            send_sem=z_send.at[way], recv_sem=tail.at[1] if h else recv.at[number(d, r), i],
             device_id=(down, up)[way], device_id_type=MESH)
 
-    def across(d, r, i):
-        q = number(d, r)
+    def across(d, r, i, h=None):
         return pltpu.make_async_remote_copy(
-            src_ref=place(0, d, r, i), dst_ref=place(0, d, 1 - r, i),
-            send_sem=x_send, recv_sem=recv.at[q, i], device_id=over, device_id_type=MESH)
-
-    def to_twin(d, r, i):
+            src_ref=place(0, d, r, i, h), dst_ref=place(0, d, 1 - r, i, h),
+            send_sem=x_send, recv_sem=tail.at[0] if h else recv.at[number(d, r), i],
+            device_id=over, device_id_type=MESH)
+
+    def to_twin(d, r, i, h=None):
         slot = slot_at(z, 0, d, r)
         later = 2 + jnp.maximum(i - early + 1, 0)
-        index = jnp.where(slot < SECOND[0], 0, jnp.where(slot == LAST, 1, later))
+        final = jnp.where(i < early, 1, 3 + count - early)
+        index = jnp.where(slot < SECOND[0], 0, jnp.where(slot == LAST, final, later))
         return pltpu.make_async_remote_copy(
-            src_ref=place(0, d, r, i), dst_ref=place(0, d, r, i), send_sem=c_send,
+            src_ref=place(0, d, r, i, h), dst_ref=place(0, d, r, i, h), send_sem=c_send,
             recv_sem=c_recv.at[index], device_id=twin, device_id_type=MESH)
 
     def to_panel(d, r, i):
@@ -157,9 +161,19 @@
             send_sem=y_send, recv_sem=y_recv.at[index],
             device_id=(here * 2 + k % 2, 1 - t), device_id_type=MESH)
 
+    def spread_panel(d, r, i):
+        pl.when(owns & (chunk(i) // 2 == part))(lambda: to_panel(d, r, i).start())
+
     def spread(d, r, i):
         to_twin(d, r, i).start()
-        pl.when(owns & (chunk(i) // 2 == part))(lambda: to_panel(d, r, i).start())
+        spread_panel(d, r, i)
+
+    def take_halves(d, i, mark):
+        for h, sem in enumerate((recv.at[number(d, 1), i], tail.at[mark])):
+            piece = all_ref.at[pl.ds(0, rows // 8), pl.ds(0, 4 * LANES)]
+            pltpu.make_async_copy(piece, piece, sem).wait()
+            to_twin(d, 1, i, h).start()
+        spread_panel(d, 1, i)
 
     def landed(sem, chunks=1):
         piece = all_ref.at[pl.ds(0, chunks * rows // 8), pl.ds(0, 8 * LANES)]
@@ -181,10 +195,17 @@
     def onward(d, r, i):
         if abs(d) == LINE - 1:
             return
-        if d < 0:
-            pl.when(has_up)(lambda: along(d, r, i, 1).start())
-        else:
-            pl.when(has_down)(lambda: along(d, r, i, 0).start())
+        way = 1 if d < 0 else 0
+        goes = has_up if way else has_down
+        if abs(d) < LINE - 2 or r == 0:
+            pl.when(goes)(lambda: along(d, r, i, way).start())
+            return
+        pl.when(goes & (i < count - 1))(lambda: along(d, r, i, way).start())
+
+        @pl.when(goes & (i == count - 1))
+        def _():
+            along(d, r, i, way, 0).start()
+            along(d, r, i, way, 1).start()
 
     def flip(i):
         for copy in inputs(i):
@@ -223,21 +244,41 @@
         def _():
             arrive(d, 0, i)
             onward(d, 0, i)
-            pl.when(i < straight(d))(lambda: across(d, 0, i).start())
+            whole = straight(d) - (1 if abs(d) == LINE - 1 else 0)
+            pl.when(i < whole)(lambda: across(d, 0, i).start())
+            if abs(d) == LINE - 1:
+                @pl.when(i == whole)
+                def _():
+                    across(d, 0, i, 0).start()
+                    across(d, 0, i, 1).start()
             spread(d, 0, i)
 
     def from_cross(d, i):
         @pl.when(exists(d) & (i >= straight(d)))
         def _():
-            arrive(d, 1, i)
-            onward(d, 1, i)
-            spread(d, 1, i)
+            def take():
+                arrive(d, 1, i)
+                onward(d, 1, i)
+                spread(d, 1, i)
+
+            if abs(d) < LINE - 1:
+                take()
+            else:
+                pl.when(i < count - 1)(take)
+                pl.when(i == count - 1)(lambda: take_halves(d, i, 1))
 
     def relayed(d, i):
         @pl.when(exists(d) & (i < straight(d)))
         def _():
-            arrive(d, 1, i)
-            spread(d, 1, i)
+            def take():
+                arrive(d, 1, i)
+                spread(d, 1, i)
+
+            if abs(d) < LINE - 1:
+                take()
+            else:
+                pl.when(i < straight(d) - 1)(take)
+                pl.when(i == straight(d) - 1)(lambda: take_halves(d, i, 0))
 
     def neighbour(i):
         arrive(0, 1, i)
@@ -254,11 +295,11 @@
         def _():
             panel_ref[:, span(slots)] = all_ref[rows_of(me % count), span(slots)]
 
-    def multiply(slots, k, add):
+    def multiply(slots, k, add, scale=None):
         product = nt_dot(all_ref[rows_of(k), span(slots)], panel_ref[:, span(slots)])
         if add:
             product += part_ref[rows_of(k), :]
-        part_ref[rows_of(k), :] = product
+        part_ref[rows_of(k), :] = product if scale is None else product * scale
 
     @pl.loop(0, count)
     def _(i):
@@ -291,8 +332,6 @@
         multiply(FIRST, chunk(i), False)
         from_line(-3, i)
         from_line(3, i)
-        from_cross(-2, i)
-        from_cross(2, i)
 
         @pl.when(end)
         def _():
@@ -301,6 +340,8 @@
 
         @pl.when(jnp.logical_not(end))
         def _():
+            from_cross(-2, i)
+            from_cross(2, i)
             later = (count + i) // 2
             pl.when(i % 2 == 0)(lambda: relayed(-1, later))
             pl.when(i % 2 == 1)(lambda: relayed(1, later))
@@ -335,6 +376,11 @@
             relayed(-3, ahead + i // 2)
             relayed(3, ahead + i // 2)
 
+        @pl.when(end & (i == 0))
+        def _():
+            from_cross(-2, count - 1)
+            from_cross(2, count - 1)
+
         @pl.when(end & ((i == 2) | (i == 4)))
         def _():
             from_cross(-3, count - 3 + i // 2)
@@ -352,8 +398,17 @@
             pl.when(end)(lambda: landed(c_recv.at[3 + i], len(SECOND)))
             multiply(SECOND, chunk(later), True)
 
-    landed(c_recv.at[1], count)
-    pl.when(jnp.logical_not(owns))(lambda: landed(y_recv.at[2], 2))
+        @pl.when(i == jnp.where(end, early - 1, count - 1))
+        def _():
+            landed(c_recv.at[1], early)
+            pl.when(jnp.logical_not(end))(lambda: landed(c_recv.at[3 + count - early], count - early))
+            columns([LAST], 2)
+
+            @pl.loop(0, READY)
+            def _(j):
+                multiply([LAST], chunk(j), True, 1.0 / total)
+
+    pl.when(end)(lambda: landed(c_recv.at[3 + count - early], count - early))
     landed(c_send, CHIPS * count)
     pl.when(owns)(lambda: landed(y_send, 2 * CHIPS))
     for zz in range(LINE):
@@ -373,7 +428,7 @@
     vmem = pl.BlockSpec(memory_space=pltpu.VMEM)
     held = hidden * tokens * 2 + width * tokens * 2 + hidden * width * 4
     return pl.pallas_call(
-        functools.partial(gather_kernel, (count, width)),
+        functools.partial(gather_kernel, (count, width, tokens)),
         out_shape=(
             pltpu.VMEM((hidden, tokens), jnp.bfloat16),
             pltpu.VMEM((width, tokens), jnp.bfloat16),
@@ -391,7 +446,8 @@
             sem(()),
             sem(()),
             sem((CHIPS, count)),
-            sem((3 + count - count // 2,)),
+            sem((2,)),
+            sem((4 + count - count // 2,)),
             sem((3,)),
         ],
         compiler_params=pltpu.CompilerParams(
@@ -400,45 +456,41 @@
     )(grad_hidden, gate)
 
 
-def finish_kernel(total, tile, all_ref, panel_ref, _, o_ref, part_ref, b_ref, sem):
-    me, t, z, x, core = position()
-    width = panel_ref.shape[0]
-    count = all_ref.shape[0] // width
+def finish_kernel(total, split, all_ref, panel_ref, _, o_ref, part_ref, sem):
+    t, width = lax.axis_index("tensor"), panel_ref.shape[0]
+    count, tile = all_ref.shape[0] // width, width // split
     lanes = pl.ds(LAST * 2 * LANES, 2 * LANES)
 
-    for ours in (True, False):
-        @pl.when((me // count == t) == ours)
-        def _():
-            rows = pl.ds(pl.multiple_of(me % count * width, width), width)
-            b_ref[...] = all_ref[rows, lanes] if ours else panel_ref[:, lanes]
-
-    def rows_of(i):
-        return pl.ds(pl.multiple_of(i * tile, tile), tile)
-
-    def out(i):
-        return pltpu.make_async_copy(part_ref.at[rows_of(i)], o_ref.at[rows_of(i)], sem.at[i])
-
-    steps = o_ref.shape[0] // tile
-
-    @pl.loop(0, steps)
-    def _(i):
-        product = nt_dot(all_ref[rows_of(i), lanes], b_ref[...])
-        part_ref[rows_of(i), :] = (part_ref[rows_of(i), :] + product) * (1.0 / total)
-        out(i).start()
-
-    @pl.loop(0, steps)
-    def _(i):
-        out(i).wait()
-
-
-def finish(everything, panel, part, tile):
+    def rows_of(j):
+        k = jnp.where(t == 0, j // split, count - 1 - j // split)
+        return pl.ds(pl.multiple_of(k * width + j % split * tile, tile), tile)
+
+    def out(j):
+        return pltpu.make_async_copy(part_ref.at[rows_of(j)], o_ref.at[rows_of(j)], sem.at[j])
+
+    @pl.loop(0, READY * split)
+    def _(j):
+        out(j).start()
+
+    @pl.loop(READY * split, count * split)
+    def _(j):
+        product = nt_dot(all_ref[rows_of(j), lanes], panel_ref[:, lanes])
+        part_ref[rows_of(j), :] = (part_ref[rows_of(j), :] + product) * (1.0 / total)
+        out(j).start()
+
+    @pl.loop(0, count * split)
+    def _(j):
+        out(j).wait()
+
+
+def finish(everything, panel, part, split):
     hidden, tokens = everything.shape
     width = panel.shape[0]
     held = hidden * tokens * 2 + width * tokens * 2 + hidden * width * 4
     keep = lambda array: pltpu.with_memory_space_constraint(array, pltpu.VMEM)
     vmem = pl.BlockSpec(memory_space=pltpu.VMEM)
     return pl.pallas_call(
-        functools.partial(finish_kernel, tokens, tile),
+        functools.partial(finish_kernel, tokens, split),
         out_shape=(
             jax.ShapeDtypeStruct((hidden, width), jnp.float32),
             pltpu.VMEM((hidden, width), jnp.float32),
@@ -447,8 +499,7 @@
         out_specs=(pl.BlockSpec(memory_space=pl.ANY), vmem),
         input_output_aliases={2: 1},
         scratch_shapes=[
-            pltpu.VMEM((width, 2 * LANES), jnp.bfloat16),
-            pltpu.SemaphoreType.DMA((hidden // tile,)),
+            pltpu.SemaphoreType.DMA((hidden // width * split,)),
         ],
         compiler_params=pltpu.CompilerParams(vmem_limit_bytes=VMEM_BYTES - held - 2**18),
     )(keep(everything), keep(panel), keep(part))[0]
@@ -467,7 +518,7 @@
     if not fits:
         return plain(grad_hidden, gate)
     everything, panel, part = gather(grad_hidden, gate, width, tokens)
-    return finish(everything, panel, part, width // 2)
+    return finish(everything, panel, part, 2)
 
 
 def solution(mesh):

time: 155 us -> 154 us (level)
  no operation moved by 1% of the time
where the time goes in v5:
time: 154 us; the launch traced here: 153 us
  Pallas kernels  153 us (99%)
    pallas_call x1, Pallas kernels, gather(): pl.pallas_call(functools.partial(gather_kernel, (count, width, tokens)),...  145 us
    pallas_call x1, Pallas kernels, finish(): pl.pallas_call(functools.partial(finish_kernel, tokens, split), out_shape...  8.69 us

profile of v5, /device:TPU:7, one launch (start us, length us, event | category | flops | bytes accessed | tf_op | source)
XLA Modules:
  0.0 153.3 jit_solution(5692678649265485399)
XLA Ops:
  0.0 144.6 %shard_map.28 = (bf16[7168,2048]{1,0:T(8,128)(2,1)S(1)}, bf16[896,2048]{1,0:T(8,128)(2,1)S(1)}, f32[7168,896]{1,0:T(8,128)S(1)}) custom-call(bf16[128,7168]{1,0:T(8,128)(2,1)} %g_ref.1, bf16[128,7168]{1,0:T(8,128)(2,1)} %v_ref.1), custom_call_target="tpu_custom_call" | custom-call | tf_op jit(solution)/shard_map/pallas_call | solution.py:430
  144.6 8.7 %shard_map.29 = (f32[7168,896]{1,0:T(8,128)}, f32[7168,896]{1,0:T(8,128)S(1)}) custom-call(bf16[7168,2048]{1,0:T(8,128)(2,1)S(1)} %get-tuple-element.9.all_ref, bf16[896,2048]{1,0:T(8,128)(2,1)S(1)} %get-tuple-element.10.panel_ref, f32[7168,896]{1,0:T(8,128)S(1)} %get-tuple-element.11._), custom_call_target="tpu_custom_call", output_to_operand_aliasing={{1}: (2, {})} | custom-call | tf_op jit(solution)/shard_map/pallas_call | solution.py:492

commit v6 on v5

--- a/solution.py
+++ b/solution.py
@@ -108,17 +108,16 @@
             for src, dst, sem in ((g_ref, g_buf, g_sem), (v_ref, v_buf, v_sem))
         ]
 
+    barrier = pltpu.get_barrier_semaphore()
+    greet = lambda dev: pl.semaphore_signal(barrier, inc=1, device_id=dev, device_id_type=MESH)
+    pl.when(has_up)(lambda: greet(up))
+    pl.when(has_down)(lambda: greet(down))
+    greet(over)
     for copy in inputs(0):
         copy.start()
-
-    barrier = pltpu.get_barrier_semaphore()
-    greet = lambda dev: pl.semaphore_signal(barrier, inc=1, device_id=dev, device_id_type=MESH)
-    greet(over)
     greet(twin)
     greet((me, 1 - t))
     greet(twin[:1] + (1 - t,))
-    pl.when(has_up)(lambda: greet(up))
-    pl.when(has_down)(lambda: greet(down))
 
     def lanes_of(slot, c):
         return pl.ds(pl.multiple_of((slot * 2 + c) * LANES, LANES), LANES)
@@ -466,7 +465,7 @@
         return pl.ds(pl.multiple_of(k * width + j % split * tile, tile), tile)
 
     def out(j):
-        return pltpu.make_async_copy(part_ref.at[rows_of(j)], o_ref.at[rows_of(j)], sem.at[j])
+        return pltpu.make_async_copy(part_ref.at[rows_of(j)], o_ref.at[rows_of(j)], sem)
 
     @pl.loop(0, READY * split)
     def _(j):
@@ -478,9 +477,7 @@
         part_ref[rows_of(j), :] = (part_ref[rows_of(j), :] + product) * (1.0 / total)
         out(j).start()
 
-    @pl.loop(0, count * split)
-    def _(j):
-        out(j).wait()
+    pltpu.make_async_copy(part_ref, o_ref, sem).wait()
 
 
 def finish(everything, panel, part, split):
@@ -499,7 +496,7 @@
         out_specs=(pl.BlockSpec(memory_space=pl.ANY), vmem),
         input_output_aliases={2: 1},
         scratch_shapes=[
-            pltpu.SemaphoreType.DMA((hidden // width * split,)),
+            pltpu.SemaphoreType.DMA(()),
         ],
         compiler_params=pltpu.CompilerParams(vmem_limit_bytes=VMEM_BYTES - held - 2**18),
     )(keep(everything), keep(panel), keep(part))[0]

time: 154 us -> 154 us (level)
  no operation moved by 1% of the time
where the time goes in v6:
time: 154 us; the launch traced here: 153 us
  Pallas kernels  153 us (99%)
    pallas_call x1, Pallas kernels, gather(): pl.pallas_call(functools.partial(gather_kernel, (count, width, tokens)),...  145 us
    pallas_call x1, Pallas kernels, finish(): pl.pallas_call(functools.partial(finish_kernel, tokens, split), out_shape...  8.56 us

profile of v6, /device:TPU:7, one launch (start us, length us, event | category | flops | bytes accessed | tf_op | source)
XLA Modules:
  0.0 153.2 jit_solution(18097430488119183497)
XLA Ops:
  0.0 144.6 %shard_map.28 = (bf16[7168,2048]{1,0:T(8,128)(2,1)S(1)}, bf16[896,2048]{1,0:T(8,128)(2,1)S(1)}, f32[7168,896]{1,0:T(8,128)S(1)}) custom-call(bf16[128,7168]{1,0:T(8,128)(2,1)} %g_ref.1, bf16[128,7168]{1,0:T(8,128)(2,1)} %v_ref.1), custom_call_target="tpu_custom_call" | custom-call | tf_op jit(solution)/shard_map/pallas_call | solution.py:429
  144.6 8.6 %shard_map.29 = (f32[7168,896]{1,0:T(8,128)}, f32[7168,896]{1,0:T(8,128)S(1)}) custom-call(bf16[7168,2048]{1,0:T(8,128)(2,1)S(1)} %get-tuple-element.9.all_ref, bf16[896,2048]{1,0:T(8,128)(2,1)S(1)} %get-tuple-element.10.panel_ref, f32[7168,896]{1,0:T(8,128)S(1)} %get-tuple-element.11._), custom_call_target="tpu_custom_call", output_to_operand_aliasing={{1}: (2, {})} | custom-call | tf_op jit(solution)/shard_map/pallas_call | solution.py:489
